TPU v7x, 512 devices: a whole 4x8x8 slice. The times are simulated.
512 devices in a mesh: dp: 32 (over x, y), mx: 4 (over z_hi, core), my: 4 (over z_lo).
Axes of the slice: x: 4, y: 8, z: 8 (z_hi: 2, z_lo: 4; z = z_hi * 4 + z_lo), core: 2. Of those that a mesh axis runs over, the one named last changes fastest.
Arguments:
- mentor_final_states: bfloat16 [2048, 4608], P('dp'), may hold values from -12 to 12
- mentor_output_matrix: bfloat16 [4608, 4096], P(None, ('mx', 'my')), may hold values from -0.09375 to 0.09375
- learner_final_states: bfloat16 [2048, 3584], P('dp', 'mx'), may hold values from -12 to 12
- learner_output_matrix: bfloat16 [3584, 4096], P('mx', 'my'), may hold values from -0.09375 to 0.09375
- loss_mask: int32 [2048], P('dp'), may hold values 0 or 1
Outputs:
- mismatch_per_piece: float32 [2048], P('dp')
- mean_loss: float32 [], replicated
- student_grad: float32 [2048, 4096], P('dp', 'my')
All inputs are finite; a program needn't handle non-finite values.
Results may differ from a plain program's by a relative error of at most 0.0003.
Values sent between devices are 32-bit elements.
No kernel may reach another device: no remote copies, remote signals or barrier semaphores. Data moves between devices by JAX's collectives and lax.ppermute only.
A program may use at most 64 MiB of HBM per device.

v0:
```python
import jax
import jax.numpy as jnp
from jax import lax
from jax.experimental import pallas as pl
from jax.experimental.pallas import tpu as pltpu
from jax.sharding import Mesh
from jax.sharding import PartitionSpec as P


DP = ("dp_0", "dp_1")
GROUP = ("zh", "co", "zl")
SOFTENING_HEAT = 2.0
SWAP = [(0, 1), (1, 0)]
LANES = 128
SUBLANES = 8
KERNEL_VMEM = 4 << 20
VMEM = pltpu.MemorySpace.VMEM
SMEM = pltpu.MemorySpace.SMEM


def teacher_route(flip):
    pairs = []
    for i in range(4):
        for j in range(4):
            zh = (j % 2) ^ flip
            pairs.append((i * 4 + j, (zh * 2 + j // 2) * 4 + i))
    return pairs


def call(kernel, outs, out_spaces, in_spaces):
    return pl.pallas_call(
        kernel,
        out_shape=outs,
        in_specs=[pl.BlockSpec(memory_space=s) for s in in_spaces],
        out_specs=[pl.BlockSpec(memory_space=s) for s in out_spaces],
        compiler_params=pltpu.CompilerParams(vmem_limit_bytes=KERNEL_VMEM),
    )


def stats_kernel(zh_ref, chip_ref, other_ref, a_ref, b_ref, stats_ref, student_ref):
    rows, width = a_ref.shape
    zh = zh_ref[0]
    for k, at in ((0, zh), (1, 1 - zh)):
        cols = pl.ds(pl.multiple_of(at * width, LANES), width)
        student_ref[:, k * width : (k + 1) * width] = (chip_ref[:, cols] + other_ref[:, cols]) * (1 / SOFTENING_HEAT)
    s_a, s_b = student_ref[:, :width], student_ref[:, width:]
    t_a, t_b = a_ref[...], b_ref[...]
    t_max = jnp.max(jnp.maximum(t_a, t_b), axis=1, keepdims=True)
    s_max = jnp.max(jnp.maximum(s_a, s_b), axis=1, keepdims=True)
    ta, tb, sa, sb = t_a - t_max, t_b - t_max, s_a - s_max, s_b - s_max
    ea, eb = jnp.exp(ta), jnp.exp(tb)
    t_sum = jnp.sum(ea + eb, axis=1, keepdims=True)
    s_sum = jnp.sum(jnp.exp(sa) + jnp.exp(sb), axis=1, keepdims=True)
    w_sum = jnp.sum(ea * (ta - sa) + eb * (tb - sb), axis=1, keepdims=True)
    lane = lax.broadcasted_iota(jnp.int32, (rows, LANES), 1)
    table = jnp.ones((rows, LANES), jnp.float32)
    for k, value in enumerate((t_max, s_max, t_sum, s_sum, w_sum)):
        table = jnp.where(lane == k, value, table)
    table = jnp.concatenate([table, jnp.ones((LANES - rows, LANES), jnp.float32)], axis=0).T
    for p in range(stats_ref.shape[0]):
        stats_ref[p] = table[:SUBLANES]


def merge_kernel(every_ref, mask_ref, mismatch_ref, sums_ref, consts_ref, mask_tile):
    rows = mask_ref.shape[1]
    tm, sm, tz, sz, w = (every_ref[:, k, :] for k in range(5))
    t_top = jnp.max(tm, axis=0, keepdims=True)
    s_top = jnp.max(sm, axis=0, keepdims=True)
    t_gap, s_gap = tm - t_top, sm - s_top
    t_scale = jnp.exp(t_gap)
    t_total = jnp.sum(tz * t_scale, axis=0, keepdims=True)
    s_total = jnp.sum(sz * jnp.exp(s_gap), axis=0, keepdims=True)
    w_total = jnp.sum(t_scale * (w + tz * (t_gap - s_gap)), axis=0, keepdims=True)
    t_log, s_log = jnp.log(t_total), jnp.log(s_total)
    mismatch = (SOFTENING_HEAT * SOFTENING_HEAT) * (w_total / t_total - t_log + s_log)
    mismatch_ref[...] = mismatch[:, :rows]
    mask_tile[...] = jnp.zeros(mask_tile.shape, jnp.float32)
    mask_tile[0:1, :rows] = mask_ref[...].astype(jnp.float32)
    importance = mask_tile[0:1, :]
    loss = jnp.sum(importance * mismatch, axis=1, keepdims=True)
    count = jnp.sum(importance, axis=1, keepdims=True)
    lane = lax.broadcasted_iota(jnp.int32, (1, LANES), 1)
    sums = jnp.where(lane == 0, loss, jnp.where(lane == 1, count, 0.0))
    sums_ref[...] = jnp.broadcast_to(sums[None], sums_ref.shape)
    row = lax.broadcasted_iota(jnp.int32, (LANES, LANES), 0)
    table = jnp.where(row == 0, t_top + t_log, jnp.where(row == 1, s_top + s_log, importance))
    consts_ref[...] = table.T[:rows]


def gap_kernel(student_ref, a_ref, b_ref, consts_ref, gap_ref):
    width = a_ref.shape[1]
    t_log, s_log = consts_ref[:, 0:1], consts_ref[:, 1:2]
    for k, ref in ((0, a_ref), (1, b_ref)):
        cols = slice(k * width, (k + 1) * width)
        gap_ref[:, cols] = jnp.exp(student_ref[:, cols] - s_log) - jnp.exp(ref[...] - t_log)


def grad_kernel(factor, place_ref, gap_ref, other_ref, sums_ref, consts_ref, grad_ref, loss_ref):
    half = gap_ref.shape[1]
    width = half // 2
    total = jnp.sum(sums_ref[...], axis=0)
    lane = lax.broadcasted_iota(jnp.int32, total.shape, 1)
    loss = jnp.sum(jnp.where(lane == 0, total, 0.0), axis=1, keepdims=True)
    count = jnp.sum(jnp.where(lane == 1, total, 0.0), axis=1, keepdims=True)
    loss_ref[...] = loss / count
    multiplier = consts_ref[:, 2:3] * (factor / count)
    core, zh = place_ref[0], place_ref[1]
    for ref, c in ((gap_ref, core), (other_ref, 1 - core)):
        for k, at in ((0, zh), (1, 1 - zh)):
            cols = pl.ds(pl.multiple_of(c * half + at * width, LANES), width)
            grad_ref[:, cols] = ref[:, k * width : (k + 1) * width] * multiplier


def local(
    mentor_final_states,
    mentor_output_matrix,
    learner_final_states,
    learner_output_matrix,
    loss_mask,
):
    tokens = mentor_final_states.shape[0]
    width = mentor_output_matrix.shape[1]
    columns = learner_output_matrix.shape[1]
    half = columns // 2
    lexicon = width * lax.axis_size(GROUP)
    rows = lax.axis_size(DP)
    peers = lax.axis_size(("co", "zl"))
    core = lax.axis_index("co")
    zh = lax.axis_index("zh")
    place = jnp.stack([core, zh]).astype(jnp.int32)
    f32 = jnp.float32

    partial = jnp.dot(learner_final_states, learner_output_matrix, preferred_element_type=f32)
    give = lax.dynamic_slice_in_dim(partial, (1 - core) * half, half, 1)
    keep = lax.dynamic_slice_in_dim(partial, core * half, half, 1)
    chip_sum = keep + lax.ppermute(give, "co", SWAP)
    other_sum = lax.ppermute(chip_sum, "zh", SWAP)

    block = jnp.dot(mentor_final_states, mentor_output_matrix, preferred_element_type=f32) / SOFTENING_HEAT
    block_a = lax.ppermute(block, GROUP, teacher_route(0))
    block_b = lax.ppermute(block, GROUP, teacher_route(1))

    stats, student = call(
        stats_kernel,
        [jax.ShapeDtypeStruct((peers, SUBLANES, LANES), f32), jax.ShapeDtypeStruct((tokens, half), f32)],
        [VMEM, VMEM],
        [SMEM, VMEM, VMEM, VMEM, VMEM],
    )(zh[None].astype(jnp.int32), chip_sum, other_sum, block_a, block_b)
    every = lax.all_to_all(stats, ("co", "zl"), 0, 0)
    mismatch, sums, consts = pl.pallas_call(
        merge_kernel,
        out_shape=[
            jax.ShapeDtypeStruct((1, tokens), f32),
            jax.ShapeDtypeStruct((rows, 1, LANES), f32),
            jax.ShapeDtypeStruct((tokens, LANES), f32),
        ],
        in_specs=[pl.BlockSpec(memory_space=VMEM)] * 2,
        out_specs=[pl.BlockSpec(memory_space=VMEM)] * 3,
        scratch_shapes=[pltpu.VMEM((SUBLANES, LANES), f32)],
        name="merge",
        compiler_params=pltpu.CompilerParams(vmem_limit_bytes=KERNEL_VMEM),
    )(every, loss_mask[None])
    all_sums = lax.all_to_all(sums, DP, 0, 0)

    (gap,) = call(
        gap_kernel, [jax.ShapeDtypeStruct((tokens, half), f32)], [VMEM], [VMEM] * 4
    )(student, block_a, block_b, consts)
    other = lax.ppermute(gap, "co", SWAP)

    def final(*refs):
        grad_kernel(SOFTENING_HEAT * lexicon * tokens * rows, *refs)

    student_grad, mean_loss = call(
        final,
        [jax.ShapeDtypeStruct((tokens, columns), f32), jax.ShapeDtypeStruct((1, 1), f32)],
        [VMEM, VMEM],
        [SMEM, VMEM, VMEM, VMEM, VMEM],
    )(place, gap, other, all_sums, consts)
    return mismatch.reshape(tokens), mean_loss.reshape(()), student_grad


def solution(mesh):
    split = Mesh(
        mesh.devices.reshape(4, 8, 2, mesh.shape["mx"] // 2, mesh.shape["my"]),
        ("dp_0", "dp_1", "zh", "co", "zl"),
    )
    mx = ("zh", "co")
    in_specs = (P(DP, None), P(None, ("zh", "co", "zl")), P(DP, mx), P(mx, "zl"), P(DP))
    out_specs = (P(DP), P(), P(DP, "zl"))

    return jax.shard_map(local, mesh=split, in_specs=in_specs, out_specs=out_specs, check_vma=False)
```

profile of v0, /device:TPU:1, one launch (start us, length us, event | category | flops | bytes accessed | tf_op | source)
XLA Modules:
  0.0 62.9 jit_solution(9254207235963097921)
XLA Ops:
  0.6 0.0 copy-start
  0.6 0.0 copy-start.2
  0.7 2.1 %fusion = f32[64,1024]{1,0:T(8,128)S(1)} fusion(bf16[64,896]{1,0:T(8,128)(2,1)} %param.7, bf16[896,1024]{1,0:T(8,128)(2,1)} %param.8), kind=kOutput, calls=%fused_computation.4 | convolution fusion | flops 117440512 | bytes 2211840 | tf_op jit(solution)/shard_map/dot_general | solution.py:133
  2.8 0.0 copy-start.1
  2.9 8.7 %collective-permute-start = (f32[64,512]{1,0:T(8,128)S(1)}, f32[64,512]{1,0:T(8,128)S(1)}, u32[]{:S(2)}, u32[]{:S(2)}) collective-permute-start(f32[64,512]{1,0:T(8,128)S(1)} %constant_dynamic-slice_fusion), channel_id=1, source_target_pairs={{0,4},{4,0},{1,5},{5,1},{2,6},{6,2},{3,7},{7,3},{8,12},{12,8},{9,1... | collective-permute-start | bytes 393224 | tf_op jit(solution)/shard_map/ppermute | solution.py:136
  11.6 1.0 %collective-permute-done = f32[64,512]{1,0:T(8,128)S(1)} collective-permute-done((f32[64,512]{1,0:T(8,128)S(1)}, f32[64,512]{1,0:T(8,128)S(1)}, u32[]{:S(2)}, u32[]{:S(2)}) %collective-permute-start) | collective-permute-done | bytes 131104 | tf_op jit(solution)/shard_map/ppermute | solution.py:136
  12.6 5.3 %collective-permute-start.1 = (f32[64,512]{1,0:T(8,128)S(1)}, f32[64,512]{1,0:T(8,128)S(1)}, u32[]{:S(2)}, u32[]{:S(2)}) collective-permute-start(f32[64,512]{1,0:T(8,128)S(1)} %dynamic-slice_add_fusion.chip_ref), channel_id=1, source_target_pairs={{0,8},{8,0},{1,9},{9,1},{2,10},{10,2},{3,11},{11,3},{4,12},{12,4},... | collective-permute-start | bytes 393224 | tf_op jit(solution)/shard_map/ppermute | solution.py:137
  17.9 0.0 copy-done
  17.9 0.0 copy-done.2
  17.9 0.5 convolution_multiply_fusion
  18.4 3.6 %collective-permute-start.2 = (f32[64,256]{1,0:T(8,128)S(1)}, f32[64,256]{1,0:T(8,128)S(1)}, u32[]{:S(2)}, u32[]{:S(2)}) collective-permute-start(f32[64,256]{1,0:T(8,128)S(1)} %convolution_multiply_fusion), channel_id=1, source_target_pairs={{0,0},{1,8},{2,4},{3,12},{4,1},{5,9},{6,5},{7,13},{8,2},{9,10},{10... | collective-permute-start | bytes 196616 | tf_op jit(solution)/shard_map/ppermute | solution.py:140
  22.1 1.9 %collective-permute-start.3 = (f32[64,256]{1,0:T(8,128)S(1)}, f32[64,256]{1,0:T(8,128)S(1)}, u32[]{:S(2)}, u32[]{:S(2)}) collective-permute-start(f32[64,256]{1,0:T(8,128)S(1)} %convolution_multiply_fusion), channel_id=1, source_target_pairs={{0,8},{1,0},{2,12},{3,4},{4,9},{5,1},{6,13},{7,5},{8,10},{9,2},{10... | collective-permute-start | bytes 196616 | tf_op jit(solution)/shard_map/ppermute | solution.py:141
  24.0 3.7 %collective-permute-done.2.a_ref = f32[64,256]{1,0:T(8,128)S(1)} collective-permute-done((f32[64,256]{1,0:T(8,128)S(1)}, f32[64,256]{1,0:T(8,128)S(1)}, u32[]{:S(2)}, u32[]{:S(2)}) %collective-permute-start.2) | collective-permute-done | bytes 65568 | tf_op jit(solution)/shard_map/ppermute | solution.py:140
  27.7 1.8 %collective-permute-done.3.b_ref = f32[64,256]{1,0:T(8,128)S(1)} collective-permute-done((f32[64,256]{1,0:T(8,128)S(1)}, f32[64,256]{1,0:T(8,128)S(1)}, u32[]{:S(2)}, u32[]{:S(2)}) %collective-permute-start.3) | collective-permute-done | bytes 65568 | tf_op jit(solution)/shard_map/ppermute | solution.py:141
  29.5 0.0 collective-permute-done.1.other_ref
  29.5 0.3 shard_map.76
  29.8 10.2 %all_to_all.10.every_ref = f32[8,8,128]{2,1,0:T(8,128)S(1)} all-to-all(f32[8,8,128]{2,1,0:T(8,128)S(1)} %get-tuple-element.10), channel_id=1, replica_groups=mesh['dp_0'=4,'dp_1'=8,'zh'=2,'co'=2,'zl'=4] {'co','zl'}, dimensions={0} | all-to-all | bytes 65536 | tf_op jit(solution)/shard_map/all_to_all | solution.py:149
  40.0 0.0 copy-done.1
  40.0 0.7 %merge.1 = (f32[1,64]{1,0:T(1,128)}, f32[32,1,128]{2,1,0:T(1,128)}, f32[64,128]{1,0:T(8,128)S(1)}) custom-call(f32[8,8,128]{2,1,0:T(8,128)S(1)} %all_to_all.10.every_ref, s32[1,64]{1,0:T(1,128)S(1)} %bitcast.9), custom_call_target="tpu_custom_call" | custom-call | tf_op jit(solution)/shard_map/merge/pallas_call | solution.py:150
  40.7 0.1 shard_map.77.refs_1_
  40.8 2.3 %collective-permute-start.4 = (f32[64,512]{1,0:T(8,128)S(1)}, f32[64,512]{1,0:T(8,128)S(1)}, u32[]{:S(2)}, u32[]{:S(2)}) collective-permute-start(f32[64,512]{1,0:T(8,128)S(1)} %shard_map.77.refs_1_), channel_id=1, source_target_pairs={{0,4},{4,0},{1,5},{5,1},{2,6},{6,2},{3,7},{7,3},{8,12},{12,8},{9,1... | collective-permute-start | bytes 393224 | tf_op jit(solution)/shard_map/ppermute | solution.py:168
  43.1 9.7 %all-to-all-start.1 = ((f32[32,1,128]{2,1,0:T(1,128)}), f32[32,1,128]{2,1,0:T(1,128)S(1)}, u32[]{:S(2)}, u32[]{:S(2)}) async-start(f32[32,1,128]{2,1,0:T(1,128)} %get-tuple-element.14), calls=%async_computation.1 | async-start | bytes 32768 | tf_op jit(solution)/shard_map/all_to_all | solution.py:163
  52.8 0.1 pad_add_fusion.refs_0_
  52.9 8.5 %all-to-all-done.1.refs_3_ = f32[32,1,128]{2,1,0:T(1,128)S(1)} async-done(((f32[32,1,128]{2,1,0:T(1,128)}), f32[32,1,128]{2,1,0:T(1,128)S(1)}, u32[]{:S(2)}, u32[]{:S(2)}) %all-to-all-start.1) | async-done | bytes 16416 | tf_op jit(solution)/shard_map/all_to_all | solution.py:163
  61.4 0.0 collective-permute-done.4.refs_2_
  61.4 1.5 %shard_map.78 = (f32[64,1024]{1,0:T(8,128)}, f32[1,1]{1,0:T(1,128)}) custom-call(s32[2]{0:T(128)S(1)} %pad_add_fusion.refs_0_, f32[64,512]{1,0:T(8,128)S(1)} %shard_map.77.refs_1_, f32[64,512]{1,0:T(8,128)S(1)} %collective-permute-done.4.refs_2_, f32[32,1,128]{2,1,0:T(1,128)S(1)} %all-to-all-done.1.refs_3_, f32[64,128]{1,0:T(8,128)S(1)} %get-tuple-element.13.consts_ref.refs_4_), custom_call_target="tpu_custom_call" | custom-call | tf_op jit(solution)/shard_map/pallas_call | solution.py:173
  (2 shorter events, 0.0 us)
Async XLA Ops:
  0.6 17.3 %copy-start = (bf16[4608,256]{1,0:T(8,128)(2,1)S(1)}, bf16[4608,256]{1,0:T(8,128)(2,1)}, u32[]{:S(2)}) copy-start(bf16[4608,256]{1,0:T(8,128)(2,1)} %param.6) | copy-start | bytes 7077892
  0.6 17.3 %copy-start.2 = (bf16[64,4608]{1,0:T(8,128)(2,1)S(1)}, bf16[64,4608]{1,0:T(8,128)(2,1)}, u32[]{:S(2)}) copy-start(bf16[64,4608]{1,0:T(8,128)(2,1)} %param.5) | copy-start | bytes 1769476
  2.8 37.2 %copy-start.1 = (s32[64]{0:T(128)S(1)}, s32[64]{0:T(128)}, u32[]{:S(2)}) copy-start(s32[64]{0:T(128)} %param.9) | copy-start | bytes 772
  2.9 9.7 %collective-permute-start = (f32[64,512]{1,0:T(8,128)S(1)}, f32[64,512]{1,0:T(8,128)S(1)}, u32[]{:S(2)}, u32[]{:S(2)}) collective-permute-start(f32[64,512]{1,0:T(8,128)S(1)} %constant_dynamic-slice_fusion), channel_id=1, source_target_pairs={{0,4},{4,0},{1,5},{5,1},{2,6},{6,2},{3,7},{7,3},{8,12},{12,8},{9,1... | collective-permute-start | bytes 393224 | tf_op jit(solution)/shard_map/ppermute | solution.py:136
  12.6 16.9 %collective-permute-start.1 = (f32[64,512]{1,0:T(8,128)S(1)}, f32[64,512]{1,0:T(8,128)S(1)}, u32[]{:S(2)}, u32[]{:S(2)}) collective-permute-start(f32[64,512]{1,0:T(8,128)S(1)} %dynamic-slice_add_fusion.chip_ref), channel_id=1, source_target_pairs={{0,8},{8,0},{1,9},{9,1},{2,10},{10,2},{3,11},{11,3},{4,12},{12,4},... | collective-permute-start | bytes 393224 | tf_op jit(solution)/shard_map/ppermute | solution.py:137
  18.4 9.3 %collective-permute-start.2 = (f32[64,256]{1,0:T(8,128)S(1)}, f32[64,256]{1,0:T(8,128)S(1)}, u32[]{:S(2)}, u32[]{:S(2)}) collective-permute-start(f32[64,256]{1,0:T(8,128)S(1)} %convolution_multiply_fusion), channel_id=1, source_target_pairs={{0,0},{1,8},{2,4},{3,12},{4,1},{5,9},{6,5},{7,13},{8,2},{9,10},{10... | collective-permute-start | bytes 196616 | tf_op jit(solution)/shard_map/ppermute | solution.py:140
  22.1 7.4 %collective-permute-start.3 = (f32[64,256]{1,0:T(8,128)S(1)}, f32[64,256]{1,0:T(8,128)S(1)}, u32[]{:S(2)}, u32[]{:S(2)}) collective-permute-start(f32[64,256]{1,0:T(8,128)S(1)} %convolution_multiply_fusion), channel_id=1, source_target_pairs={{0,8},{1,0},{2,12},{3,4},{4,9},{5,1},{6,13},{7,5},{8,10},{9,2},{10... | collective-permute-start | bytes 196616 | tf_op jit(solution)/shard_map/ppermute | solution.py:141
  40.8 20.6 %collective-permute-start.4 = (f32[64,512]{1,0:T(8,128)S(1)}, f32[64,512]{1,0:T(8,128)S(1)}, u32[]{:S(2)}, u32[]{:S(2)}) collective-permute-start(f32[64,512]{1,0:T(8,128)S(1)} %shard_map.77.refs_1_), channel_id=1, source_target_pairs={{0,4},{4,0},{1,5},{5,1},{2,6},{6,2},{3,7},{7,3},{8,12},{12,8},{9,1... | collective-permute-start | bytes 393224 | tf_op jit(solution)/shard_map/ppermute | solution.py:168
  43.1 18.3 %all-to-all-start.1 = ((f32[32,1,128]{2,1,0:T(1,128)}), f32[32,1,128]{2,1,0:T(1,128)S(1)}, u32[]{:S(2)}, u32[]{:S(2)}) async-start(f32[32,1,128]{2,1,0:T(1,128)} %get-tuple-element.14), calls=%async_computation.1 | async-start | bytes 32768 | tf_op jit(solution)/shard_map/all_to_all | solution.py:163
where the time goes:
time: 63.2 us; the launch traced here: 62.9 us
  starting transfers between devices  31.6 us (50%)
  waiting for transfers between devices  15 us (24%)
  blocking collectives  10.2 us (16%)
  matrix products  2.68 us (4%)
  Pallas kernels  2.55 us (4%)
  between operations  0.77 us (1%)
    all_to_all x1, blocking collectives, local(): every = lax.all_to_all(stats, ('co', 'zl'), 0, 0)  10.2 us
    all_to_all x1, starting transfers between devices, local(): all_sums = lax.all_to_all(sums, DP, 0, 0)  9.69 us
    ppermute x1, starting transfers between devices, local(): chip_sum = keep + lax.ppermute(give, 'co', SWAP)  8.75 us
    all_to_all x1, waiting for transfers between devices, local(): all_sums = lax.all_to_all(sums, DP, 0, 0)  8.52 us
    ppermute x1, starting transfers between devices, local(): other_sum = lax.ppermute(chip_sum, 'zh', SWAP)  5.29 us
    ppermute x1, waiting for transfers between devices, local(): block_a = lax.ppermute(block, GROUP, teacher_route(0))  3.71 us
    ppermute x1, starting transfers between devices, local(): block_a = lax.ppermute(block, GROUP, teacher_route(0))  3.63 us
    ppermute x1, starting transfers between devices, local(): other = lax.ppermute(gap, 'co', SWAP)  2.3 us
  transfers between devices with their start and end apart: 6, of which 4 were waited for; matrix products, arithmetic and copies ran while one was open for 1% of the time, Pallas kernels for 0%

commit v1 on v0

--- a/solution.py
+++ b/solution.py
@@ -37,21 +37,18 @@
     )
 
 
-def stats_kernel(zh_ref, chip_ref, other_ref, a_ref, b_ref, stats_ref, student_ref):
+def stats_kernel(zh_ref, chip_ref, other_ref, a_ref, stats_ref):
     rows, width = a_ref.shape
-    zh = zh_ref[0]
-    for k, at in ((0, zh), (1, 1 - zh)):
-        cols = pl.ds(pl.multiple_of(at * width, LANES), width)
-        student_ref[:, k * width : (k + 1) * width] = (chip_ref[:, cols] + other_ref[:, cols]) * (1 / SOFTENING_HEAT)
-    s_a, s_b = student_ref[:, :width], student_ref[:, width:]
-    t_a, t_b = a_ref[...], b_ref[...]
-    t_max = jnp.max(jnp.maximum(t_a, t_b), axis=1, keepdims=True)
-    s_max = jnp.max(jnp.maximum(s_a, s_b), axis=1, keepdims=True)
-    ta, tb, sa, sb = t_a - t_max, t_b - t_max, s_a - s_max, s_b - s_max
-    ea, eb = jnp.exp(ta), jnp.exp(tb)
-    t_sum = jnp.sum(ea + eb, axis=1, keepdims=True)
-    s_sum = jnp.sum(jnp.exp(sa) + jnp.exp(sb), axis=1, keepdims=True)
-    w_sum = jnp.sum(ea * (ta - sa) + eb * (tb - sb), axis=1, keepdims=True)
+    cols = pl.ds(pl.multiple_of(zh_ref[0] * width, LANES), width)
+    s = (chip_ref[:, cols] + other_ref[:, cols]) * (1 / SOFTENING_HEAT)
+    t = a_ref[...]
+    t_max = jnp.max(t, axis=1, keepdims=True)
+    s_max = jnp.max(s, axis=1, keepdims=True)
+    t, s = t - t_max, s - s_max
+    e = jnp.exp(t)
+    t_sum = jnp.sum(e, axis=1, keepdims=True)
+    s_sum = jnp.sum(jnp.exp(s), axis=1, keepdims=True)
+    w_sum = jnp.sum(e * (t - s), axis=1, keepdims=True)
     lane = lax.broadcasted_iota(jnp.int32, (rows, LANES), 1)
     table = jnp.ones((rows, LANES), jnp.float32)
     for k, value in enumerate((t_max, s_max, t_sum, s_sum, w_sum)):
@@ -87,12 +84,14 @@
     consts_ref[...] = table.T[:rows]
 
 
-def gap_kernel(student_ref, a_ref, b_ref, consts_ref, gap_ref):
+def gap_kernel(zh_ref, chip_ref, other_ref, a_ref, b_ref, consts_ref, gap_ref):
     width = a_ref.shape[1]
+    zh = zh_ref[0]
     t_log, s_log = consts_ref[:, 0:1], consts_ref[:, 1:2]
-    for k, ref in ((0, a_ref), (1, b_ref)):
-        cols = slice(k * width, (k + 1) * width)
-        gap_ref[:, cols] = jnp.exp(student_ref[:, cols] - s_log) - jnp.exp(ref[...] - t_log)
+    for k, at, ref in ((0, zh, a_ref), (1, 1 - zh, b_ref)):
+        cols = pl.ds(pl.multiple_of(at * width, LANES), width)
+        student = (chip_ref[:, cols] + other_ref[:, cols]) * (1 / SOFTENING_HEAT)
+        gap_ref[:, k * width : (k + 1) * width] = jnp.exp(student - s_log) - jnp.exp(ref[...] - t_log)
 
 
 def grad_kernel(factor, place_ref, gap_ref, other_ref, sums_ref, consts_ref, grad_ref, loss_ref):
@@ -124,9 +123,10 @@
     half = columns // 2
     lexicon = width * lax.axis_size(GROUP)
     rows = lax.axis_size(DP)
-    peers = lax.axis_size(("co", "zl"))
+    peers = lax.axis_size(GROUP)
     core = lax.axis_index("co")
     zh = lax.axis_index("zh")
+    zh_at = zh[None].astype(jnp.int32)
     place = jnp.stack([core, zh]).astype(jnp.int32)
     f32 = jnp.float32
 
@@ -140,13 +140,10 @@
     block_a = lax.ppermute(block, GROUP, teacher_route(0))
     block_b = lax.ppermute(block, GROUP, teacher_route(1))
 
-    stats, student = call(
-        stats_kernel,
-        [jax.ShapeDtypeStruct((peers, SUBLANES, LANES), f32), jax.ShapeDtypeStruct((tokens, half), f32)],
-        [VMEM, VMEM],
-        [SMEM, VMEM, VMEM, VMEM, VMEM],
-    )(zh[None].astype(jnp.int32), chip_sum, other_sum, block_a, block_b)
-    every = lax.all_to_all(stats, ("co", "zl"), 0, 0)
+    (stats,) = call(
+        stats_kernel, [jax.ShapeDtypeStruct((peers, SUBLANES, LANES), f32)], [VMEM], [SMEM, VMEM, VMEM, VMEM]
+    )(zh_at, chip_sum, other_sum, block_a)
+    every = lax.all_to_all(stats, GROUP, 0, 0)
     mismatch, sums, consts = pl.pallas_call(
         merge_kernel,
         out_shape=[
@@ -163,8 +160,8 @@
     all_sums = lax.all_to_all(sums, DP, 0, 0)
 
     (gap,) = call(
-        gap_kernel, [jax.ShapeDtypeStruct((tokens, half), f32)], [VMEM], [VMEM] * 4
-    )(student, block_a, block_b, consts)
+        gap_kernel, [jax.ShapeDtypeStruct((tokens, half), f32)], [VMEM], [SMEM] + [VMEM] * 5
+    )(zh_at, chip_sum, other_sum, block_a, block_b, consts)
     other = lax.ppermute(gap, "co", SWAP)
 
     def final(*refs):

time: 63.2 us -> 66.3 us (1.049)
  starting transfers between devices: 31.6 us -> 43.8 us
  blocking collectives: 10.2 us -> 0 us
    all_to_all x1 -> x0, blocking collectives: 10.2 us -> none  [local(): every = lax.all_to_all(stats, ('co', 'zl'), 0, 0)]
    all_to_all x0 -> x1, starting transfers between devices: none -> 6.65 us  [local(): every = lax.all_to_all(stats, GROUP, 0, 0)]
    ppermute x1, starting transfers between devices: 1.93 us -> 6.54 us  [local(): block_b = lax.ppermute(block, GROUP, teacher_route(1))]
    ppermute x1, waiting for transfers between devices: 1.76 us -> 0.03 us  [local(): block_b = lax.ppermute(block, GROUP, teacher_route(1))]
    ppermute x1, waiting for transfers between devices: 3.71 us -> 4.89 us  [local(): block_a = lax.ppermute(block, GROUP, teacher_route(0))]
    all_to_all x0 -> x1, waiting for transfers between devices: none -> 1.04 us  [local(): every = lax.all_to_all(stats, GROUP, 0, 0)]
    ppermute x1, starting transfers between devices: 2.3 us -> 3.26 us  [local(): other = lax.ppermute(gap, 'co', SWAP)]
  transfers between devices with their start and end apart: 6 -> 7, of which waited for: 4 -> 4; matrix products, arithmetic and copies ran while one was open for 1% -> 1% of each run, Pallas kernels for 0% -> 1%
where the time goes in v1:
time: 66.3 us; the launch traced here: 66 us
  starting transfers between devices  43.8 us (66%)
  waiting for transfers between devices  15.4 us (23%)
  Pallas kernels  3.2 us (5%)
  matrix products  2.68 us (4%)
  between operations  0.76 us (1%)
    all_to_all x1, starting transfers between devices, local(): all_sums = lax.all_to_all(sums, DP, 0, 0)  9.66 us
    ppermute x1, starting transfers between devices, local(): chip_sum = keep + lax.ppermute(give, 'co', SWAP)  8.75 us
    all_to_all x1, waiting for transfers between devices, local(): all_sums = lax.all_to_all(sums, DP, 0, 0)  8.51 us
    all_to_all x1, starting transfers between devices, local(): every = lax.all_to_all(stats, GROUP, 0, 0)  6.65 us
    ppermute x1, starting transfers between devices, local(): block_b = lax.ppermute(block, GROUP, teacher_route(1))  6.54 us
    ppermute x1, starting transfers between devices, local(): other_sum = lax.ppermute(chip_sum, 'zh', SWAP)  5.29 us
    ppermute x1, waiting for transfers between devices, local(): block_a = lax.ppermute(block, GROUP, teacher_route(0))  4.89 us
    ppermute x1, starting transfers between devices, local(): block_a = lax.ppermute(block, GROUP, teacher_route(0))  3.63 us
  transfers between devices with their start and end apart: 7, of which 4 were waited for; matrix products, arithmetic and copies ran while one was open for 1% of the time, Pallas kernels for 1%

profile of v1, /device:TPU:1, one launch (start us, length us, event | category | flops | bytes accessed | tf_op | source)
XLA Modules:
  0.0 66.0 jit_solution(1981829438548758475)
XLA Ops:
  0.6 0.0 copy-start
  0.6 0.0 copy-start.2
  0.7 2.1 %fusion = f32[64,1024]{1,0:T(8,128)S(1)} fusion(bf16[64,896]{1,0:T(8,128)(2,1)} %param.7, bf16[896,1024]{1,0:T(8,128)(2,1)} %param.8), kind=kOutput, calls=%fused_computation.4 | convolution fusion | flops 117440512 | bytes 2211840 | tf_op jit(solution)/shard_map/dot_general | solution.py:133
  2.8 0.0 copy-start.1
  2.9 8.7 %collective-permute-start = (f32[64,512]{1,0:T(8,128)S(1)}, f32[64,512]{1,0:T(8,128)S(1)}, u32[]{:S(2)}, u32[]{:S(2)}) collective-permute-start(f32[64,512]{1,0:T(8,128)S(1)} %constant_dynamic-slice_fusion), channel_id=1, source_target_pairs={{0,4},{4,0},{1,5},{5,1},{2,6},{6,2},{3,7},{7,3},{8,12},{12,8},{9,1... | collective-permute-start | bytes 393224 | tf_op jit(solution)/shard_map/ppermute | solution.py:136
  11.6 1.0 %collective-permute-done = f32[64,512]{1,0:T(8,128)S(1)} collective-permute-done((f32[64,512]{1,0:T(8,128)S(1)}, f32[64,512]{1,0:T(8,128)S(1)}, u32[]{:S(2)}, u32[]{:S(2)}) %collective-permute-start) | collective-permute-done | bytes 131104 | tf_op jit(solution)/shard_map/ppermute | solution.py:136
  12.6 5.3 %collective-permute-start.1 = (f32[64,512]{1,0:T(8,128)S(1)}, f32[64,512]{1,0:T(8,128)S(1)}, u32[]{:S(2)}, u32[]{:S(2)}) collective-permute-start(f32[64,512]{1,0:T(8,128)S(1)} %dynamic-slice_add_fusion.chip_ref), channel_id=1, source_target_pairs={{0,8},{8,0},{1,9},{9,1},{2,10},{10,2},{3,11},{11,3},{4,12},{12,4},... | collective-permute-start | bytes 393224 | tf_op jit(solution)/shard_map/ppermute | solution.py:137
  17.9 0.0 copy-done
  17.9 0.0 copy-done.2
  17.9 0.5 convolution_multiply_fusion
  18.4 3.6 %collective-permute-start.2 = (f32[64,256]{1,0:T(8,128)S(1)}, f32[64,256]{1,0:T(8,128)S(1)}, u32[]{:S(2)}, u32[]{:S(2)}) collective-permute-start(f32[64,256]{1,0:T(8,128)S(1)} %convolution_multiply_fusion), channel_id=1, source_target_pairs={{0,0},{1,8},{2,4},{3,12},{4,1},{5,9},{6,5},{7,13},{8,2},{9,10},{10... | collective-permute-start | bytes 196616 | tf_op jit(solution)/shard_map/ppermute | solution.py:140
  22.1 4.9 %collective-permute-done.2.a_ref = f32[64,256]{1,0:T(8,128)S(1)} collective-permute-done((f32[64,256]{1,0:T(8,128)S(1)}, f32[64,256]{1,0:T(8,128)S(1)}, u32[]{:S(2)}, u32[]{:S(2)}) %collective-permute-start.2) | collective-permute-done | bytes 65568 | tf_op jit(solution)/shard_map/ppermute | solution.py:140
  27.0 0.0 collective-permute-done.1.other_ref
  27.0 0.9 %shard_map.76 = f32[16,8,128]{2,1,0:T(8,128)} custom-call(s32[1]{0:T(128)} %bitcast.zh_ref, f32[64,512]{1,0:T(8,128)S(1)} %dynamic-slice_add_fusion.chip_ref, f32[64,512]{1,0:T(8,128)S(1)} %collective-permute-done.1.other_ref, f32[64,256]{1,0:T(8,128)S(1)} %collective-permute-done.2.a_ref), custom_call_target="tpu_custom_call" | custom-call | tf_op jit(solution)/shard_map/pallas_call | solution.py:143
  27.9 6.6 %all-to-all-start = ((f32[16,8,128]{2,1,0:T(8,128)}), f32[16,8,128]{2,1,0:T(8,128)S(1)}, u32[]{:S(2)}, u32[]{:S(2)}) async-start(f32[16,8,128]{2,1,0:T(8,128)} %shard_map.76), calls=%async_computation | async-start | bytes 131072 | tf_op jit(solution)/shard_map/all_to_all | solution.py:146
  34.5 6.5 %collective-permute-start.3 = (f32[64,256]{1,0:T(8,128)S(1)}, f32[64,256]{1,0:T(8,128)S(1)}, u32[]{:S(2)}, u32[]{:S(2)}) collective-permute-start(f32[64,256]{1,0:T(8,128)S(1)} %convolution_multiply_fusion), channel_id=1, source_target_pairs={{0,8},{1,0},{2,12},{3,4},{4,9},{5,1},{6,13},{7,5},{8,10},{9,2},{10... | collective-permute-start | bytes 196616 | tf_op jit(solution)/shard_map/ppermute | solution.py:141
  41.1 1.0 %all-to-all-done.every_ref = f32[16,8,128]{2,1,0:T(8,128)S(1)} async-done(((f32[16,8,128]{2,1,0:T(8,128)}), f32[16,8,128]{2,1,0:T(8,128)S(1)}, u32[]{:S(2)}, u32[]{:S(2)}) %all-to-all-start) | async-done | bytes 65568 | tf_op jit(solution)/shard_map/all_to_all | solution.py:146
  42.1 0.0 copy-done.1
  42.1 0.7 %merge.1 = (f32[1,64]{1,0:T(1,128)}, f32[32,1,128]{2,1,0:T(1,128)}, f32[64,128]{1,0:T(8,128)S(1)}) custom-call(f32[16,8,128]{2,1,0:T(8,128)S(1)} %all-to-all-done.every_ref, s32[1,64]{1,0:T(1,128)S(1)} %bitcast.9), custom_call_target="tpu_custom_call" | custom-call | tf_op jit(solution)/shard_map/merge/pallas_call | solution.py:147
  42.9 0.0 collective-permute-done.3.b_ref
  42.9 0.1 shard_map.77.refs_1_
  43.0 3.3 %collective-permute-start.4 = (f32[64,512]{1,0:T(8,128)S(1)}, f32[64,512]{1,0:T(8,128)S(1)}, u32[]{:S(2)}, u32[]{:S(2)}) collective-permute-start(f32[64,512]{1,0:T(8,128)S(1)} %shard_map.77.refs_1_), channel_id=1, source_target_pairs={{0,4},{4,0},{1,5},{5,1},{2,6},{6,2},{3,7},{7,3},{8,12},{12,8},{9,1... | collective-permute-start | bytes 393224 | tf_op jit(solution)/shard_map/ppermute | solution.py:165
  46.3 9.7 %all-to-all-start.1 = ((f32[32,1,128]{2,1,0:T(1,128)}), f32[32,1,128]{2,1,0:T(1,128)S(1)}, u32[]{:S(2)}, u32[]{:S(2)}) async-start(f32[32,1,128]{2,1,0:T(1,128)} %get-tuple-element.10), calls=%async_computation.1 | async-start | bytes 32768 | tf_op jit(solution)/shard_map/all_to_all | solution.py:160
  55.9 0.1 pad_add_fusion.refs_0_
  56.0 8.5 %all-to-all-done.1.refs_3_ = f32[32,1,128]{2,1,0:T(1,128)S(1)} async-done(((f32[32,1,128]{2,1,0:T(1,128)}), f32[32,1,128]{2,1,0:T(1,128)S(1)}, u32[]{:S(2)}, u32[]{:S(2)}) %all-to-all-start.1) | async-done | bytes 16416 | tf_op jit(solution)/shard_map/all_to_all | solution.py:160
  64.5 0.0 collective-permute-done.4.refs_2_
  64.5 1.5 %shard_map.78 = (f32[64,1024]{1,0:T(8,128)}, f32[1,1]{1,0:T(1,128)}) custom-call(s32[2]{0:T(128)S(1)} %pad_add_fusion.refs_0_, f32[64,512]{1,0:T(8,128)S(1)} %shard_map.77.refs_1_, f32[64,512]{1,0:T(8,128)S(1)} %collective-permute-done.4.refs_2_, f32[32,1,128]{2,1,0:T(1,128)S(1)} %all-to-all-done.1.refs_3_, f32[64,128]{1,0:T(8,128)S(1)} %get-tuple-element.9.consts_ref.refs_4_), custom_call_target="tpu_custom_call" | custom-call | tf_op jit(solution)/shard_map/pallas_call | solution.py:170
  (2 shorter events, 0.0 us)
Async XLA Ops:
  0.6 17.3 %copy-start = (bf16[4608,256]{1,0:T(8,128)(2,1)S(1)}, bf16[4608,256]{1,0:T(8,128)(2,1)}, u32[]{:S(2)}) copy-start(bf16[4608,256]{1,0:T(8,128)(2,1)} %param.6) | copy-start | bytes 7077892
  0.6 17.3 %copy-start.2 = (bf16[64,4608]{1,0:T(8,128)(2,1)S(1)}, bf16[64,4608]{1,0:T(8,128)(2,1)}, u32[]{:S(2)}) copy-start(bf16[64,4608]{1,0:T(8,128)(2,1)} %param.5) | copy-start | bytes 1769476
  2.8 39.3 %copy-start.1 = (s32[64]{0:T(128)S(1)}, s32[64]{0:T(128)}, u32[]{:S(2)}) copy-start(s32[64]{0:T(128)} %param.9) | copy-start | bytes 772
  2.9 9.7 %collective-permute-start = (f32[64,512]{1,0:T(8,128)S(1)}, f32[64,512]{1,0:T(8,128)S(1)}, u32[]{:S(2)}, u32[]{:S(2)}) collective-permute-start(f32[64,512]{1,0:T(8,128)S(1)} %constant_dynamic-slice_fusion), channel_id=1, source_target_pairs={{0,4},{4,0},{1,5},{5,1},{2,6},{6,2},{3,7},{7,3},{8,12},{12,8},{9,1... | collective-permute-start | bytes 393224 | tf_op jit(solution)/shard_map/ppermute | solution.py:136
  12.6 14.4 %collective-permute-start.1 = (f32[64,512]{1,0:T(8,128)S(1)}, f32[64,512]{1,0:T(8,128)S(1)}, u32[]{:S(2)}, u32[]{:S(2)}) collective-permute-start(f32[64,512]{1,0:T(8,128)S(1)} %dynamic-slice_add_fusion.chip_ref), channel_id=1, source_target_pairs={{0,8},{8,0},{1,9},{9,1},{2,10},{10,2},{3,11},{11,3},{4,12},{12,4},... | collective-permute-start | bytes 393224 | tf_op jit(solution)/shard_map/ppermute | solution.py:137
  18.4 8.5 %collective-permute-start.2 = (f32[64,256]{1,0:T(8,128)S(1)}, f32[64,256]{1,0:T(8,128)S(1)}, u32[]{:S(2)}, u32[]{:S(2)}) collective-permute-start(f32[64,256]{1,0:T(8,128)S(1)} %convolution_multiply_fusion), channel_id=1, source_target_pairs={{0,0},{1,8},{2,4},{3,12},{4,1},{5,9},{6,5},{7,13},{8,2},{9,10},{10... | collective-permute-start | bytes 196616 | tf_op jit(solution)/shard_map/ppermute | solution.py:140
  27.9 14.2 %all-to-all-start = ((f32[16,8,128]{2,1,0:T(8,128)}), f32[16,8,128]{2,1,0:T(8,128)S(1)}, u32[]{:S(2)}, u32[]{:S(2)}) async-start(f32[16,8,128]{2,1,0:T(8,128)} %shard_map.76), calls=%async_computation | async-start | bytes 131072 | tf_op jit(solution)/shard_map/all_to_all | solution.py:146
  34.5 8.4 %collective-permute-start.3 = (f32[64,256]{1,0:T(8,128)S(1)}, f32[64,256]{1,0:T(8,128)S(1)}, u32[]{:S(2)}, u32[]{:S(2)}) collective-permute-start(f32[64,256]{1,0:T(8,128)S(1)} %convolution_multiply_fusion), channel_id=1, source_target_pairs={{0,8},{1,0},{2,12},{3,4},{4,9},{5,1},{6,13},{7,5},{8,10},{9,2},{10... | collective-permute-start | bytes 196616 | tf_op jit(solution)/shard_map/ppermute | solution.py:141
  43.0 21.5 %collective-permute-start.4 = (f32[64,512]{1,0:T(8,128)S(1)}, f32[64,512]{1,0:T(8,128)S(1)}, u32[]{:S(2)}, u32[]{:S(2)}) collective-permute-start(f32[64,512]{1,0:T(8,128)S(1)} %shard_map.77.refs_1_), channel_id=1, source_target_pairs={{0,4},{4,0},{1,5},{5,1},{2,6},{6,2},{3,7},{7,3},{8,12},{12,8},{9,1... | collective-permute-start | bytes 393224 | tf_op jit(solution)/shard_map/ppermute | solution.py:165
  46.3 18.3 %all-to-all-start.1 = ((f32[32,1,128]{2,1,0:T(1,128)}), f32[32,1,128]{2,1,0:T(1,128)S(1)}, u32[]{:S(2)}, u32[]{:S(2)}) async-start(f32[32,1,128]{2,1,0:T(1,128)} %get-tuple-element.10), calls=%async_computation.1 | async-start | bytes 32768 | tf_op jit(solution)/shard_map/all_to_all | solution.py:160

commit v2 on v1

--- a/solution.py
+++ b/solution.py
@@ -19,12 +19,7 @@
 
 
 def teacher_route(flip):
-    pairs = []
-    for i in range(4):
-        for j in range(4):
-            zh = (j % 2) ^ flip
-            pairs.append((i * 4 + j, (zh * 2 + j // 2) * 4 + i))
-    return pairs
+    return [(i * 4 + j, (((j // 2) ^ flip) * 2 + j % 2) * 4 + i) for i in range(4) for j in range(4)]
 
 
 def call(kernel, outs, out_spaces, in_spaces):
@@ -35,6 +30,15 @@
         out_specs=[pl.BlockSpec(memory_space=s) for s in out_spaces],
         compiler_params=pltpu.CompilerParams(vmem_limit_bytes=KERNEL_VMEM),
     )
+
+
+def split_kernel(core_ref, partial_ref, give_ref, keep_ref):
+    width = give_ref.shape[1] // 2
+    core = core_ref[0]
+    for ref, c in ((give_ref, 1 - core), (keep_ref, core)):
+        for z in range(2):
+            cols = pl.ds(pl.multiple_of((2 * z + c) * width, LANES), width)
+            ref[:, z * width : (z + 1) * width] = partial_ref[:, cols]
 
 
 def stats_kernel(zh_ref, chip_ref, other_ref, a_ref, stats_ref):
@@ -95,8 +99,7 @@
 
 
 def grad_kernel(factor, place_ref, gap_ref, other_ref, sums_ref, consts_ref, grad_ref, loss_ref):
-    half = gap_ref.shape[1]
-    width = half // 2
+    width = gap_ref.shape[1] // 2
     total = jnp.sum(sums_ref[...], axis=0)
     lane = lax.broadcasted_iota(jnp.int32, total.shape, 1)
     loss = jnp.sum(jnp.where(lane == 0, total, 0.0), axis=1, keepdims=True)
@@ -106,7 +109,7 @@
     core, zh = place_ref[0], place_ref[1]
     for ref, c in ((gap_ref, core), (other_ref, 1 - core)):
         for k, at in ((0, zh), (1, 1 - zh)):
-            cols = pl.ds(pl.multiple_of(c * half + at * width, LANES), width)
+            cols = pl.ds(pl.multiple_of((2 * at + c) * width, LANES), width)
             grad_ref[:, cols] = ref[:, k * width : (k + 1) * width] * multiplier
 
 
@@ -130,9 +133,11 @@
     place = jnp.stack([core, zh]).astype(jnp.int32)
     f32 = jnp.float32
 
+    core_at = core[None].astype(jnp.int32)
     partial = jnp.dot(learner_final_states, learner_output_matrix, preferred_element_type=f32)
-    give = lax.dynamic_slice_in_dim(partial, (1 - core) * half, half, 1)
-    keep = lax.dynamic_slice_in_dim(partial, core * half, half, 1)
+    give, keep = call(
+        split_kernel, [jax.ShapeDtypeStruct((tokens, half), f32)] * 2, [VMEM] * 2, [SMEM, VMEM]
+    )(core_at, partial)
     chip_sum = keep + lax.ppermute(give, "co", SWAP)
     other_sum = lax.ppermute(chip_sum, "zh", SWAP)
 

time: 66.3 us -> 67.6 us (1.020)
  starting transfers between devices: 43.8 us -> 45.7 us
    all_to_all x1, starting transfers between devices: 6.65 us -> 7.99 us  [local(): every = lax.all_to_all(stats, GROUP, 0, 0)]
where the time goes in v2:
time: 67.6 us; the launch traced here: 67.3 us
  starting transfers between devices  45.7 us (68%)
  waiting for transfers between devices  14.8 us (22%)
  Pallas kernels  3.22 us (5%)
  matrix products  2.67 us (4%)
  between operations  0.76 us (1%)
    all_to_all x1, starting transfers between devices, local(): all_sums = lax.all_to_all(sums, DP, 0, 0)  9.66 us
    ppermute x1, starting transfers between devices, local(): chip_sum = keep + lax.ppermute(give, 'co', SWAP)  8.75 us
    all_to_all x1, waiting for transfers between devices, local(): all_sums = lax.all_to_all(sums, DP, 0, 0)  8.51 us
    all_to_all x1, starting transfers between devices, local(): every = lax.all_to_all(stats, GROUP, 0, 0)  7.99 us
    ppermute x1, starting transfers between devices, local(): block_b = lax.ppermute(block, GROUP, teacher_route(1))  6.54 us
    ppermute x1, starting transfers between devices, local(): other_sum = lax.ppermute(chip_sum, 'zh', SWAP)  5.29 us
    ppermute x1, waiting for transfers between devices, local(): block_a = lax.ppermute(block, GROUP, teacher_route(0))  4.25 us
    ppermute x1, starting transfers between devices, local(): other = lax.ppermute(gap, 'co', SWAP)  3.87 us
  transfers between devices with their start and end apart: 7, of which 4 were waited for; matrix products, arithmetic and copies ran while one was open for 1% of the time, Pallas kernels for 1%

profile of v2, /device:TPU:1, one launch (start us, length us, event | category | flops | bytes accessed | tf_op | source)
XLA Modules:
  0.0 67.3 jit_solution(10351688184865287682)
XLA Ops:
  0.6 0.0 copy-start
  0.6 0.0 copy-start.2
  0.7 2.1 %fusion.partial_ref = f32[64,1024]{1,0:T(8,128)S(1)} fusion(bf16[64,896]{1,0:T(8,128)(2,1)} %param.7, bf16[896,1024]{1,0:T(8,128)(2,1)} %param.8), kind=kOutput, calls=%fused_computation.2 | convolution fusion | flops 117440512 | bytes 2211840 | tf_op jit(solution)/shard_map/dot_general | solution.py:137
  2.8 0.0 copy-start.1
  2.9 8.7 %collective-permute-start = (f32[64,512]{1,0:T(8,128)S(1)}, f32[64,512]{1,0:T(8,128)S(1)}, u32[]{:S(2)}, u32[]{:S(2)}) collective-permute-start(f32[64,512]{1,0:T(8,128)S(1)} %get-tuple-element.11), channel_id=1, source_target_pairs={{0,4},{4,0},{1,5},{5,1},{2,6},{6,2},{3,7},{7,3},{8,12},{12,8},{9,1... | collective-permute-start | bytes 393224 | tf_op jit(solution)/shard_map/ppermute | solution.py:141
  11.6 1.0 %collective-permute-done = f32[64,512]{1,0:T(8,128)S(1)} collective-permute-done((f32[64,512]{1,0:T(8,128)S(1)}, f32[64,512]{1,0:T(8,128)S(1)}, u32[]{:S(2)}, u32[]{:S(2)}) %collective-permute-start) | collective-permute-done | bytes 131104 | tf_op jit(solution)/shard_map/ppermute | solution.py:141
  12.6 5.3 %collective-permute-start.1 = (f32[64,512]{1,0:T(8,128)S(1)}, f32[64,512]{1,0:T(8,128)S(1)}, u32[]{:S(2)}, u32[]{:S(2)}) collective-permute-start(f32[64,512]{1,0:T(8,128)S(1)} %add.3.chip_ref), channel_id=1, source_target_pairs={{0,8},{8,0},{1,9},{9,1},{2,10},{10,2},{3,11},{11,3},{4,12},{12,4},... | collective-permute-start | bytes 393224 | tf_op jit(solution)/shard_map/ppermute | solution.py:142
  17.9 0.0 copy-done
  17.9 0.0 copy-done.2
  17.9 0.5 convolution_multiply_fusion
  18.4 3.6 %collective-permute-start.2 = (f32[64,256]{1,0:T(8,128)S(1)}, f32[64,256]{1,0:T(8,128)S(1)}, u32[]{:S(2)}, u32[]{:S(2)}) collective-permute-start(f32[64,256]{1,0:T(8,128)S(1)} %convolution_multiply_fusion), channel_id=1, source_target_pairs={{0,0},{1,4},{2,8},{3,12},{4,1},{5,5},{6,9},{7,13},{8,2},{9,6},{10,... | collective-permute-start | bytes 196616 | tf_op jit(solution)/shard_map/ppermute | solution.py:145
  22.1 4.2 %collective-permute-done.2.a_ref = f32[64,256]{1,0:T(8,128)S(1)} collective-permute-done((f32[64,256]{1,0:T(8,128)S(1)}, f32[64,256]{1,0:T(8,128)S(1)}, u32[]{:S(2)}, u32[]{:S(2)}) %collective-permute-start.2) | collective-permute-done | bytes 65568 | tf_op jit(solution)/shard_map/ppermute | solution.py:145
  26.3 0.0 collective-permute-done.1.other_ref
  26.3 0.9 %shard_map.77 = f32[16,8,128]{2,1,0:T(8,128)} custom-call(s32[1]{0:T(128)} %bitcast.zh_ref, f32[64,512]{1,0:T(8,128)S(1)} %add.3.chip_ref, f32[64,512]{1,0:T(8,128)S(1)} %collective-permute-done.1.other_ref, f32[64,256]{1,0:T(8,128)S(1)} %collective-permute-done.2.a_ref), custom_call_target="tpu_custom_call" | custom-call | tf_op jit(solution)/shard_map/pallas_call | solution.py:148
  27.2 8.0 %all-to-all-start = ((f32[16,8,128]{2,1,0:T(8,128)}), f32[16,8,128]{2,1,0:T(8,128)S(1)}, u32[]{:S(2)}, u32[]{:S(2)}) async-start(f32[16,8,128]{2,1,0:T(8,128)} %shard_map.77), calls=%async_computation | async-start | bytes 131072 | tf_op jit(solution)/shard_map/all_to_all | solution.py:151
  35.2 6.5 %collective-permute-start.3 = (f32[64,256]{1,0:T(8,128)S(1)}, f32[64,256]{1,0:T(8,128)S(1)}, u32[]{:S(2)}, u32[]{:S(2)}) collective-permute-start(f32[64,256]{1,0:T(8,128)S(1)} %convolution_multiply_fusion), channel_id=1, source_target_pairs={{0,8},{1,12},{2,0},{3,4},{4,9},{5,13},{6,1},{7,5},{8,10},{9,14},{1... | collective-permute-start | bytes 196616 | tf_op jit(solution)/shard_map/ppermute | solution.py:146
  41.8 1.0 %all-to-all-done.every_ref = f32[16,8,128]{2,1,0:T(8,128)S(1)} async-done(((f32[16,8,128]{2,1,0:T(8,128)}), f32[16,8,128]{2,1,0:T(8,128)S(1)}, u32[]{:S(2)}, u32[]{:S(2)}) %all-to-all-start) | async-done | bytes 65568 | tf_op jit(solution)/shard_map/all_to_all | solution.py:151
  42.8 0.0 copy-done.1
  42.8 0.7 %merge.1 = (f32[1,64]{1,0:T(1,128)}, f32[32,1,128]{2,1,0:T(1,128)}, f32[64,128]{1,0:T(8,128)S(1)}) custom-call(f32[16,8,128]{2,1,0:T(8,128)S(1)} %all-to-all-done.every_ref, s32[1,64]{1,0:T(1,128)S(1)} %bitcast.9), custom_call_target="tpu_custom_call" | custom-call | tf_op jit(solution)/shard_map/merge/pallas_call | solution.py:152
  43.6 0.0 collective-permute-done.3.b_ref
  43.6 0.1 shard_map.78.refs_1_
  43.7 3.9 %collective-permute-start.4 = (f32[64,512]{1,0:T(8,128)S(1)}, f32[64,512]{1,0:T(8,128)S(1)}, u32[]{:S(2)}, u32[]{:S(2)}) collective-permute-start(f32[64,512]{1,0:T(8,128)S(1)} %shard_map.78.refs_1_), channel_id=1, source_target_pairs={{0,4},{4,0},{1,5},{5,1},{2,6},{6,2},{3,7},{7,3},{8,12},{12,8},{9,1... | collective-permute-start | bytes 393224 | tf_op jit(solution)/shard_map/ppermute | solution.py:170
  47.6 9.7 %all-to-all-start.1 = ((f32[32,1,128]{2,1,0:T(1,128)}), f32[32,1,128]{2,1,0:T(1,128)S(1)}, u32[]{:S(2)}, u32[]{:S(2)}) async-start(f32[32,1,128]{2,1,0:T(1,128)} %get-tuple-element.14), calls=%async_computation.1 | async-start | bytes 32768 | tf_op jit(solution)/shard_map/all_to_all | solution.py:165
  57.3 0.1 pad_add_fusion.refs_0_
  57.3 8.5 %all-to-all-done.1.refs_3_ = f32[32,1,128]{2,1,0:T(1,128)S(1)} async-done(((f32[32,1,128]{2,1,0:T(1,128)}), f32[32,1,128]{2,1,0:T(1,128)S(1)}, u32[]{:S(2)}, u32[]{:S(2)}) %all-to-all-start.1) | async-done | bytes 16416 | tf_op jit(solution)/shard_map/all_to_all | solution.py:165
  65.8 0.0 collective-permute-done.4.refs_2_
  65.9 1.5 %shard_map.79 = (f32[64,1024]{1,0:T(8,128)}, f32[1,1]{1,0:T(1,128)}) custom-call(s32[2]{0:T(128)S(1)} %pad_add_fusion.refs_0_, f32[64,512]{1,0:T(8,128)S(1)} %shard_map.78.refs_1_, f32[64,512]{1,0:T(8,128)S(1)} %collective-permute-done.4.refs_2_, f32[32,1,128]{2,1,0:T(1,128)S(1)} %all-to-all-done.1.refs_3_, f32[64,128]{1,0:T(8,128)S(1)} %get-tuple-element.13.consts_ref.refs_4_), custom_call_target="tpu_custom_call" | custom-call | tf_op jit(solution)/shard_map/pallas_call | solution.py:175
  (2 shorter events, 0.0 us)
Async XLA Ops:
  0.6 17.3 %copy-start = (bf16[4608,256]{1,0:T(8,128)(2,1)S(1)}, bf16[4608,256]{1,0:T(8,128)(2,1)}, u32[]{:S(2)}) copy-start(bf16[4608,256]{1,0:T(8,128)(2,1)} %param.6) | copy-start | bytes 7077892
  0.6 17.3 %copy-start.2 = (bf16[64,4608]{1,0:T(8,128)(2,1)S(1)}, bf16[64,4608]{1,0:T(8,128)(2,1)}, u32[]{:S(2)}) copy-start(bf16[64,4608]{1,0:T(8,128)(2,1)} %param.5) | copy-start | bytes 1769476
  2.8 40.0 %copy-start.1 = (s32[64]{0:T(128)S(1)}, s32[64]{0:T(128)}, u32[]{:S(2)}) copy-start(s32[64]{0:T(128)} %param.9) | copy-start | bytes 772
  2.9 9.7 %collective-permute-start = (f32[64,512]{1,0:T(8,128)S(1)}, f32[64,512]{1,0:T(8,128)S(1)}, u32[]{:S(2)}, u32[]{:S(2)}) collective-permute-start(f32[64,512]{1,0:T(8,128)S(1)} %get-tuple-element.11), channel_id=1, source_target_pairs={{0,4},{4,0},{1,5},{5,1},{2,6},{6,2},{3,7},{7,3},{8,12},{12,8},{9,1... | collective-permute-start | bytes 393224 | tf_op jit(solution)/shard_map/ppermute | solution.py:141
  12.6 13.7 %collective-permute-start.1 = (f32[64,512]{1,0:T(8,128)S(1)}, f32[64,512]{1,0:T(8,128)S(1)}, u32[]{:S(2)}, u32[]{:S(2)}) collective-permute-start(f32[64,512]{1,0:T(8,128)S(1)} %add.3.chip_ref), channel_id=1, source_target_pairs={{0,8},{8,0},{1,9},{9,1},{2,10},{10,2},{3,11},{11,3},{4,12},{12,4},... | collective-permute-start | bytes 393224 | tf_op jit(solution)/shard_map/ppermute | solution.py:142
  18.4 7.9 %collective-permute-start.2 = (f32[64,256]{1,0:T(8,128)S(1)}, f32[64,256]{1,0:T(8,128)S(1)}, u32[]{:S(2)}, u32[]{:S(2)}) collective-permute-start(f32[64,256]{1,0:T(8,128)S(1)} %convolution_multiply_fusion), channel_id=1, source_target_pairs={{0,0},{1,4},{2,8},{3,12},{4,1},{5,5},{6,9},{7,13},{8,2},{9,6},{10,... | collective-permute-start | bytes 196616 | tf_op jit(solution)/shard_map/ppermute | solution.py:145
  27.2 15.6 %all-to-all-start = ((f32[16,8,128]{2,1,0:T(8,128)}), f32[16,8,128]{2,1,0:T(8,128)S(1)}, u32[]{:S(2)}, u32[]{:S(2)}) async-start(f32[16,8,128]{2,1,0:T(8,128)} %shard_map.77), calls=%async_computation | async-start | bytes 131072 | tf_op jit(solution)/shard_map/all_to_all | solution.py:151
  35.2 8.4 %collective-permute-start.3 = (f32[64,256]{1,0:T(8,128)S(1)}, f32[64,256]{1,0:T(8,128)S(1)}, u32[]{:S(2)}, u32[]{:S(2)}) collective-permute-start(f32[64,256]{1,0:T(8,128)S(1)} %convolution_multiply_fusion), channel_id=1, source_target_pairs={{0,8},{1,12},{2,0},{3,4},{4,9},{5,13},{6,1},{7,5},{8,10},{9,14},{1... | collective-permute-start | bytes 196616 | tf_op jit(solution)/shard_map/ppermute | solution.py:146
  43.7 22.1 %collective-permute-start.4 = (f32[64,512]{1,0:T(8,128)S(1)}, f32[64,512]{1,0:T(8,128)S(1)}, u32[]{:S(2)}, u32[]{:S(2)}) collective-permute-start(f32[64,512]{1,0:T(8,128)S(1)} %shard_map.78.refs_1_), channel_id=1, source_target_pairs={{0,4},{4,0},{1,5},{5,1},{2,6},{6,2},{3,7},{7,3},{8,12},{12,8},{9,1... | collective-permute-start | bytes 393224 | tf_op jit(solution)/shard_map/ppermute | solution.py:170
  47.6 18.3 %all-to-all-start.1 = ((f32[32,1,128]{2,1,0:T(1,128)}), f32[32,1,128]{2,1,0:T(1,128)S(1)}, u32[]{:S(2)}, u32[]{:S(2)}) async-start(f32[32,1,128]{2,1,0:T(1,128)} %get-tuple-element.14), calls=%async_computation.1 | async-start | bytes 32768 | tf_op jit(solution)/shard_map/all_to_all | solution.py:165

commit v3 on v0

--- a/solution.py
+++ b/solution.py
@@ -95,7 +95,7 @@
         gap_ref[:, cols] = jnp.exp(student_ref[:, cols] - s_log) - jnp.exp(ref[...] - t_log)
 
 
-def grad_kernel(factor, place_ref, gap_ref, other_ref, sums_ref, consts_ref, grad_ref, loss_ref):
+def grad_kernel(factor, core_ref, zh_ref, gap_ref, other_ref, sums_ref, consts_ref, grad_ref, loss_ref):
     half = gap_ref.shape[1]
     width = half // 2
     total = jnp.sum(sums_ref[...], axis=0)
@@ -104,7 +104,7 @@
     count = jnp.sum(jnp.where(lane == 1, total, 0.0), axis=1, keepdims=True)
     loss_ref[...] = loss / count
     multiplier = consts_ref[:, 2:3] * (factor / count)
-    core, zh = place_ref[0], place_ref[1]
+    core, zh = core_ref[0], zh_ref[0]
     for ref, c in ((gap_ref, core), (other_ref, 1 - core)):
         for k, at in ((0, zh), (1, 1 - zh)):
             cols = pl.ds(pl.multiple_of(c * half + at * width, LANES), width)
@@ -127,13 +127,17 @@
     peers = lax.axis_size(("co", "zl"))
     core = lax.axis_index("co")
     zh = lax.axis_index("zh")
-    place = jnp.stack([core, zh]).astype(jnp.int32)
+    core_at, zh_at = core[None].astype(jnp.int32), zh[None].astype(jnp.int32)
     f32 = jnp.float32
 
-    partial = jnp.dot(learner_final_states, learner_output_matrix, preferred_element_type=f32)
-    give = lax.dynamic_slice_in_dim(partial, (1 - core) * half, half, 1)
-    keep = lax.dynamic_slice_in_dim(partial, core * half, half, 1)
-    chip_sum = keep + lax.ppermute(give, "co", SWAP)
+    def product(c):
+        matrix = lax.dynamic_slice_in_dim(learner_output_matrix, c * half, half, 1)
+        return jnp.dot(learner_final_states, matrix, preferred_element_type=f32)
+
+    give = product(1 - core)
+    from_core = lax.ppermute(give, "co", SWAP)
+    keep = lax.optimization_barrier(product(core))
+    chip_sum = keep + from_core
     other_sum = lax.ppermute(chip_sum, "zh", SWAP)
 
     block = jnp.dot(mentor_final_states, mentor_output_matrix, preferred_element_type=f32) / SOFTENING_HEAT
@@ -145,7 +149,7 @@
         [jax.ShapeDtypeStruct((peers, SUBLANES, LANES), f32), jax.ShapeDtypeStruct((tokens, half), f32)],
         [VMEM, VMEM],
         [SMEM, VMEM, VMEM, VMEM, VMEM],
-    )(zh[None].astype(jnp.int32), chip_sum, other_sum, block_a, block_b)
+    )(zh_at, chip_sum, other_sum, block_a, block_b)
     every = lax.all_to_all(stats, ("co", "zl"), 0, 0)
     mismatch, sums, consts = pl.pallas_call(
         merge_kernel,
@@ -174,8 +178,8 @@
         final,
         [jax.ShapeDtypeStruct((tokens, columns), f32), jax.ShapeDtypeStruct((1, 1), f32)],
         [VMEM, VMEM],
-        [SMEM, VMEM, VMEM, VMEM, VMEM],
-    )(place, gap, other, all_sums, consts)
+        [SMEM, SMEM, VMEM, VMEM, VMEM, VMEM],
+    )(core_at, zh_at, gap, other, all_sums, consts)
     return mismatch.reshape(tokens), mean_loss.reshape(()), student_grad
 
 

time: 63.2 us -> 62.1 us (0.983)
  blocking collectives: 10.2 us -> 29.1 us
  waiting for transfers between devices: 15 us -> 4.23 us
  starting transfers between devices: 31.6 us -> 22.1 us
  matrix products: 2.68 us -> 3.72 us
  Pallas kernels: 2.55 us -> 1.83 us
    all_to_all x0 -> x1, blocking collectives: none -> 18.1 us  [local(): all_sums = lax.all_to_all(sums, DP, 0, 0)]
    all_to_all x1 -> x0, starting transfers between devices: 9.69 us -> none  [local(): all_sums = lax.all_to_all(sums, DP, 0, 0)]
    all_to_all x1 -> x0, waiting for transfers between devices: 8.52 us -> none  [local(): all_sums = lax.all_to_all(sums, DP, 0, 0)]
    ppermute x1, waiting for transfers between devices: 3.71 us -> 1.31 us  [local(): block_a = lax.ppermute(block, GROUP, teacher_route(0))]
    ppermute x1, waiting for transfers between devices: 1.76 us -> 2.92 us  [local(): block_b = lax.ppermute(block, GROUP, teacher_route(1))]
    dot_general x1 -> x2, matrix products: 2.14 us -> 3.19 us  [product(): return jnp.dot(learner_final_states, matrix, preferred_element_type=f32)]
    ppermute x1, waiting for transfers between devices: 0.96 us -> 0.01 us  [local(): from_core = lax.ppermute(give, 'co', SWAP)]
    all_to_all x1, blocking collectives: 10.2 us -> 11 us  [local(): every = lax.all_to_all(stats, ('co', 'zl'), 0, 0)]
  transfers between devices with their start and end apart: 6 -> 5, of which waited for: 4 -> 2; matrix products, arithmetic and copies ran while one was open for 1% -> 3% of each run, Pallas kernels for 0% -> 0%
where the time goes in v3:
time: 62.1 us; the launch traced here: 61.8 us
  blocking collectives  29.1 us (47%)
  starting transfers between devices  22.1 us (36%)
  waiting for transfers between devices  4.23 us (7%)
  matrix products  3.72 us (6%)
  Pallas kernels  1.83 us (3%)
  between operations  0.77 us (1%)
    all_to_all x1, blocking collectives, local(): all_sums = lax.all_to_all(sums, DP, 0, 0)  18.1 us
    all_to_all x1, blocking collectives, local(): every = lax.all_to_all(stats, ('co', 'zl'), 0, 0)  11 us
    ppermute x1, starting transfers between devices, local(): from_core = lax.ppermute(give, 'co', SWAP)  8.75 us
    ppermute x1, starting transfers between devices, local(): other_sum = lax.ppermute(chip_sum, 'zh', SWAP)  5.29 us
    ppermute x1, starting transfers between devices, local(): block_a = lax.ppermute(block, GROUP, teacher_route(0))  3.82 us
    dot_general x2, matrix products, product(): return jnp.dot(learner_final_states, matrix, preferred_element_type=f32)  3.19 us
    ppermute x1, waiting for transfers between devices, local(): block_b = lax.ppermute(block, GROUP, teacher_route(1))  2.92 us
    ppermute x1, starting transfers between devices, local(): other = lax.ppermute(gap, 'co', SWAP)  2.3 us
  transfers between devices with their start and end apart: 5, of which 2 were waited for; matrix products, arithmetic and copies ran while one was open for 3% of the time, Pallas kernels for 0%

profile of v3, /device:TPU:1, one launch (start us, length us, event | category | flops | bytes accessed | tf_op | source)
XLA Modules:
  0.0 61.8 jit_solution(2563362987437730108)
XLA Ops:
  0.6 0.0 copy-start
  0.6 0.0 copy-start.2
  0.7 1.7 %convolution_bitcast_fusion = f32[64,512]{1,0:T(8,128)S(1)} fusion(bf16[64,896]{1,0:T(8,128)(2,1)} %param.7, bf16[896,1024]{1,0:T(8,128)(2,1)} %param.8, s32[]{:T(128)S(6)} %select_n.7), kind=kOutput, calls=%fused_computation | convolution fusion | flops 58720256 | bytes 1163268 | tf_op jit(solution)/shard_map/dot_general | solution.py:135
  2.3 8.7 %collective-permute-start = (f32[64,512]{1,0:T(8,128)S(1)}, f32[64,512]{1,0:T(8,128)S(1)}, u32[]{:S(2)}, u32[]{:S(2)}) collective-permute-start(f32[64,512]{1,0:T(8,128)S(1)} %convolution_bitcast_fusion), channel_id=1, source_target_pairs={{0,4},{4,0},{1,5},{5,1},{2,6},{6,2},{3,7},{7,3},{8,12},{12,8},{9,1... | collective-permute-start | bytes 393224 | tf_op jit(solution)/shard_map/ppermute | solution.py:138
  11.1 1.5 %convolution_bitcast_fusion.1 = f32[64,512]{1,0:T(8,128)S(1)} fusion(bf16[64,896]{1,0:T(8,128)(2,1)} %param.7, bf16[896,1024]{1,0:T(8,128)(2,1)} %param.8, s32[]{:T(128)S(6)} %select_n.6), kind=kOutput, calls=%fused_computation.1 | convolution fusion | flops 58720256 | bytes 1163268 | tf_op jit(solution)/shard_map/dot_general | solution.py:135
  12.6 0.0 collective-permute-done
  12.7 0.0 copy-start.1
  12.7 5.3 %collective-permute-start.1 = (f32[64,512]{1,0:T(8,128)S(1)}, f32[64,512]{1,0:T(8,128)S(1)}, u32[]{:S(2)}, u32[]{:S(2)}) collective-permute-start(f32[64,512]{1,0:T(8,128)S(1)} %add.11.chip_ref), channel_id=1, source_target_pairs={{0,8},{8,0},{1,9},{9,1},{2,10},{10,2},{3,11},{11,3},{4,12},{12,4},... | collective-permute-start | bytes 393224 | tf_op jit(solution)/shard_map/ppermute | solution.py:141
  18.0 0.0 copy-done
  18.0 0.0 copy-done.2
  18.0 0.5 convolution_multiply_fusion
  18.5 1.9 %collective-permute-start.3 = (f32[64,256]{1,0:T(8,128)S(1)}, f32[64,256]{1,0:T(8,128)S(1)}, u32[]{:S(2)}, u32[]{:S(2)}) collective-permute-start(f32[64,256]{1,0:T(8,128)S(1)} %convolution_multiply_fusion), channel_id=1, source_target_pairs={{0,8},{1,0},{2,12},{3,4},{4,9},{5,1},{6,13},{7,5},{8,10},{9,2},{10... | collective-permute-start | bytes 196616 | tf_op jit(solution)/shard_map/ppermute | solution.py:145
  20.4 3.8 %collective-permute-start.2 = (f32[64,256]{1,0:T(8,128)S(1)}, f32[64,256]{1,0:T(8,128)S(1)}, u32[]{:S(2)}, u32[]{:S(2)}) collective-permute-start(f32[64,256]{1,0:T(8,128)S(1)} %convolution_multiply_fusion), channel_id=1, source_target_pairs={{0,0},{1,8},{2,4},{3,12},{4,1},{5,9},{6,5},{7,13},{8,2},{9,10},{10... | collective-permute-start | bytes 196616 | tf_op jit(solution)/shard_map/ppermute | solution.py:144
  24.3 2.9 %collective-permute-done.3.b_ref = f32[64,256]{1,0:T(8,128)S(1)} collective-permute-done((f32[64,256]{1,0:T(8,128)S(1)}, f32[64,256]{1,0:T(8,128)S(1)}, u32[]{:S(2)}, u32[]{:S(2)}) %collective-permute-start.3) | collective-permute-done | bytes 65568 | tf_op jit(solution)/shard_map/ppermute | solution.py:145
  27.2 1.3 %collective-permute-done.2.a_ref = f32[64,256]{1,0:T(8,128)S(1)} collective-permute-done((f32[64,256]{1,0:T(8,128)S(1)}, f32[64,256]{1,0:T(8,128)S(1)}, u32[]{:S(2)}, u32[]{:S(2)}) %collective-permute-start.2) | collective-permute-done | bytes 65568 | tf_op jit(solution)/shard_map/ppermute | solution.py:144
  28.5 0.0 collective-permute-done.1.other_ref
  28.5 0.3 shard_map.76
  28.8 11.0 %all_to_all.10.every_ref = f32[8,8,128]{2,1,0:T(8,128)S(1)} all-to-all(f32[8,8,128]{2,1,0:T(8,128)S(1)} %get-tuple-element.10), channel_id=1, replica_groups=mesh['dp_0'=4,'dp_1'=8,'zh'=2,'co'=2,'zl'=4] {'co','zl'}, dimensions={0} | all-to-all | bytes 65536 | tf_op jit(solution)/shard_map/all_to_all | solution.py:153
  39.8 0.0 copy-done.1
  39.8 0.6 merge.1
  40.3 0.1 shard_map.77.refs_2_
  40.4 2.3 %collective-permute-start.4 = (f32[64,512]{1,0:T(8,128)S(1)}, f32[64,512]{1,0:T(8,128)S(1)}, u32[]{:S(2)}, u32[]{:S(2)}) collective-permute-start(f32[64,512]{1,0:T(8,128)S(1)} %shard_map.77.refs_2_), channel_id=1, source_target_pairs={{0,4},{4,0},{1,5},{5,1},{2,6},{6,2},{3,7},{7,3},{8,12},{12,8},{9,1... | collective-permute-start | bytes 393224 | tf_op jit(solution)/shard_map/ppermute | solution.py:172
  42.7 18.1 %all_to_all.11.refs_4_ = f32[32,1,128]{2,1,0:T(1,128)S(1)} all-to-all(f32[32,1,128]{2,1,0:T(1,128)S(1)} %get-tuple-element.14), channel_id=1, replica_groups=mesh['dp_0'=4,'dp_1'=8,'zh'=2,'co'=2,'zl'=4] {'dp_0','dp_1'}, dimensions={0} | all-to-all | bytes 32768 | tf_op jit(solution)/shard_map/all_to_all | solution.py:167
  60.9 0.0 collective-permute-done.4.refs_3_
  60.9 0.9 %shard_map.78 = (f32[64,1024]{1,0:T(8,128)}, f32[1,1]{1,0:T(1,128)}) custom-call(s32[1]{0:T(128)} %bitcast.5.refs_0_, s32[1]{0:T(128)} %bitcast.zh_ref.refs_1_, f32[64,512]{1,0:T(8,128)S(1)} %shard_map.77.refs_2_, f32[64,512]{1,0:T(8,128)S(1)} %collective-permute-done.4.refs_3_, f32[32,1,128]{2,1,0:T(1,128)S(1)} %all_to_all.11.refs_4_, ...), custom_call_target="tpu_custom_call" | custom-call | tf_op jit(solution)/shard_map/pallas_call | solution.py:177
  (1 shorter events, 0.0 us)
Async XLA Ops:
  0.6 17.3 %copy-start = (bf16[4608,256]{1,0:T(8,128)(2,1)S(1)}, bf16[4608,256]{1,0:T(8,128)(2,1)}, u32[]{:S(2)}) copy-start(bf16[4608,256]{1,0:T(8,128)(2,1)} %param.6) | copy-start | bytes 7077892
  0.6 17.3 %copy-start.2 = (bf16[64,4608]{1,0:T(8,128)(2,1)S(1)}, bf16[64,4608]{1,0:T(8,128)(2,1)}, u32[]{:S(2)}) copy-start(bf16[64,4608]{1,0:T(8,128)(2,1)} %param.5) | copy-start | bytes 1769476
  2.3 10.3 %collective-permute-start = (f32[64,512]{1,0:T(8,128)S(1)}, f32[64,512]{1,0:T(8,128)S(1)}, u32[]{:S(2)}, u32[]{:S(2)}) collective-permute-start(f32[64,512]{1,0:T(8,128)S(1)} %convolution_bitcast_fusion), channel_id=1, source_target_pairs={{0,4},{4,0},{1,5},{5,1},{2,6},{6,2},{3,7},{7,3},{8,12},{12,8},{9,1... | collective-permute-start | bytes 393224 | tf_op jit(solution)/shard_map/ppermute | solution.py:138
  12.7 27.1 %copy-start.1 = (s32[64]{0:T(128)S(1)}, s32[64]{0:T(128)}, u32[]{:S(2)}) copy-start(s32[64]{0:T(128)} %param.9) | copy-start | bytes 772
  12.7 15.8 %collective-permute-start.1 = (f32[64,512]{1,0:T(8,128)S(1)}, f32[64,512]{1,0:T(8,128)S(1)}, u32[]{:S(2)}, u32[]{:S(2)}) collective-permute-start(f32[64,512]{1,0:T(8,128)S(1)} %add.11.chip_ref), channel_id=1, source_target_pairs={{0,8},{8,0},{1,9},{9,1},{2,10},{10,2},{3,11},{11,3},{4,12},{12,4},... | collective-permute-start | bytes 393224 | tf_op jit(solution)/shard_map/ppermute | solution.py:141
  18.5 8.7 %collective-permute-start.3 = (f32[64,256]{1,0:T(8,128)S(1)}, f32[64,256]{1,0:T(8,128)S(1)}, u32[]{:S(2)}, u32[]{:S(2)}) collective-permute-start(f32[64,256]{1,0:T(8,128)S(1)} %convolution_multiply_fusion), channel_id=1, source_target_pairs={{0,8},{1,0},{2,12},{3,4},{4,9},{5,1},{6,13},{7,5},{8,10},{9,2},{10... | collective-permute-start | bytes 196616 | tf_op jit(solution)/shard_map/ppermute | solution.py:145
  20.4 8.1 %collective-permute-start.2 = (f32[64,256]{1,0:T(8,128)S(1)}, f32[64,256]{1,0:T(8,128)S(1)}, u32[]{:S(2)}, u32[]{:S(2)}) collective-permute-start(f32[64,256]{1,0:T(8,128)S(1)} %convolution_multiply_fusion), channel_id=1, source_target_pairs={{0,0},{1,8},{2,4},{3,12},{4,1},{5,9},{6,5},{7,13},{8,2},{9,10},{10... | collective-permute-start | bytes 196616 | tf_op jit(solution)/shard_map/ppermute | solution.py:144
  40.4 20.5 %collective-permute-start.4 = (f32[64,512]{1,0:T(8,128)S(1)}, f32[64,512]{1,0:T(8,128)S(1)}, u32[]{:S(2)}, u32[]{:S(2)}) collective-permute-start(f32[64,512]{1,0:T(8,128)S(1)} %shard_map.77.refs_2_), channel_id=1, source_target_pairs={{0,4},{4,0},{1,5},{5,1},{2,6},{6,2},{3,7},{7,3},{8,12},{12,8},{9,1... | collective-permute-start | bytes 393224 | tf_op jit(solution)/shard_map/ppermute | solution.py:172

commit v4 on v3

--- a/solution.py
+++ b/solution.py
@@ -7,7 +7,8 @@
 from jax.sharding import PartitionSpec as P
 
 
-DP = ("dp_0", "dp_1")
+DP = "dp"
+SERVED = [22, 31, 20, 30, 4, 28, 15, 21, 29, 7, 12, 23, 0, 26, 11, 6, 13, 10, 5, 27, 19, 14, 9, 18, 3, 17, 25, 2, 16, 24, 8, 1]
 GROUP = ("zh", "co", "zl")
 SOFTENING_HEAT = 2.0
 SWAP = [(0, 1), (1, 0)]
@@ -150,7 +151,7 @@
         [VMEM, VMEM],
         [SMEM, VMEM, VMEM, VMEM, VMEM],
     )(zh_at, chip_sum, other_sum, block_a, block_b)
-    every = lax.all_to_all(stats, ("co", "zl"), 0, 0)
+    every = lax.all_to_all(stats, ("zl", "co"), 0, 0)
     mismatch, sums, consts = pl.pallas_call(
         merge_kernel,
         out_shape=[
@@ -164,7 +165,7 @@
         name="merge",
         compiler_params=pltpu.CompilerParams(vmem_limit_bytes=KERNEL_VMEM),
     )(every, loss_mask[None])
-    all_sums = lax.all_to_all(sums, DP, 0, 0)
+    all_sums = lax.all_to_all(sums, DP, 0, 0, axis_index_groups=[SERVED])
 
     (gap,) = call(
         gap_kernel, [jax.ShapeDtypeStruct((tokens, half), f32)], [VMEM], [VMEM] * 4
@@ -185,8 +186,8 @@
 
 def solution(mesh):
     split = Mesh(
-        mesh.devices.reshape(4, 8, 2, mesh.shape["mx"] // 2, mesh.shape["my"]),
-        ("dp_0", "dp_1", "zh", "co", "zl"),
+        mesh.devices.reshape(mesh.shape["dp"], 2, mesh.shape["mx"] // 2, mesh.shape["my"]),
+        ("dp", "zh", "co", "zl"),
     )
     mx = ("zh", "co")
     in_specs = (P(DP, None), P(None, ("zh", "co", "zl")), P(DP, mx), P(mx, "zl"), P(DP))

time: 62.1 us -> 57.4 us (0.924)
  blocking collectives: 29.1 us -> 24 us
    all_to_all x2, blocking collectives: 29.1 us -> 24 us  [the longest x1 13.5 us: local(): all_sums = lax.all_to_all(sums, DP, 0, 0, axis_index_groups=[SERVED])]
  transfers between devices with their start and end apart: 5 -> 5, of which waited for: 2 -> 2; matrix products, arithmetic and copies ran while one was open for 3% -> 4% of each run, Pallas kernels for 0% -> 0%
where the time goes in v4:
time: 57.4 us; the launch traced here: 57.1 us
  blocking collectives  24 us (42%)
  starting transfers between devices  22.5 us (39%)
  waiting for transfers between devices  4.23 us (7%)
  matrix products  3.72 us (6%)
  Pallas kernels  1.83 us (3%)
  between operations  0.77 us (1%)
    all_to_all x1, blocking collectives, local(): all_sums = lax.all_to_all(sums, DP, 0, 0, axis_index_groups=[SERVED])  13.5 us
    all_to_all x1, blocking collectives, local(): every = lax.all_to_all(stats, ('zl', 'co'), 0, 0)  10.6 us
    ppermute x1, starting transfers between devices, local(): from_core = lax.ppermute(give, 'co', SWAP)  8.75 us
    ppermute x1, starting transfers between devices, local(): other_sum = lax.ppermute(chip_sum, 'zh', SWAP)  5.29 us
    ppermute x1, starting transfers between devices, local(): block_a = lax.ppermute(block, GROUP, teacher_route(0))  3.82 us
    dot_general x2, matrix products, product(): return jnp.dot(learner_final_states, matrix, preferred_element_type=f32)  3.19 us
    ppermute x1, waiting for transfers between devices, local(): block_b = lax.ppermute(block, GROUP, teacher_route(1))  2.92 us
    ppermute x1, starting transfers between devices, local(): other = lax.ppermute(gap, 'co', SWAP)  2.69 us
  transfers between devices with their start and end apart: 5, of which 2 were waited for; matrix products, arithmetic and copies ran while one was open for 4% of the time, Pallas kernels for 0%

profile of v4, /device:TPU:1, one launch (start us, length us, event | category | flops | bytes accessed | tf_op | source)
XLA Modules:
  0.0 57.1 jit_solution(3422750087222567831)
XLA Ops:
  0.6 0.0 copy-start
  0.6 0.0 copy-start.2
  0.7 1.7 %convolution_bitcast_fusion = f32[64,512]{1,0:T(8,128)S(1)} fusion(bf16[64,896]{1,0:T(8,128)(2,1)} %param.7, bf16[896,1024]{1,0:T(8,128)(2,1)} %param.8, s32[]{:T(128)S(6)} %select_n.7), kind=kOutput, calls=%fused_computation | convolution fusion | flops 58720256 | bytes 1163268 | tf_op jit(solution)/shard_map/dot_general | solution.py:136
  2.3 8.7 %collective-permute-start = (f32[64,512]{1,0:T(8,128)S(1)}, f32[64,512]{1,0:T(8,128)S(1)}, u32[]{:S(2)}, u32[]{:S(2)}) collective-permute-start(f32[64,512]{1,0:T(8,128)S(1)} %convolution_bitcast_fusion), channel_id=1, source_target_pairs={{0,4},{4,0},{1,5},{5,1},{2,6},{6,2},{3,7},{7,3},{8,12},{12,8},{9,1... | collective-permute-start | bytes 393224 | tf_op jit(solution)/shard_map/ppermute | solution.py:139
  11.1 1.5 %convolution_bitcast_fusion.1 = f32[64,512]{1,0:T(8,128)S(1)} fusion(bf16[64,896]{1,0:T(8,128)(2,1)} %param.7, bf16[896,1024]{1,0:T(8,128)(2,1)} %param.8, s32[]{:T(128)S(6)} %select_n.6), kind=kOutput, calls=%fused_computation.1 | convolution fusion | flops 58720256 | bytes 1163268 | tf_op jit(solution)/shard_map/dot_general | solution.py:136
  12.6 0.0 collective-permute-done
  12.7 0.0 copy-start.1
  12.7 5.3 %collective-permute-start.1 = (f32[64,512]{1,0:T(8,128)S(1)}, f32[64,512]{1,0:T(8,128)S(1)}, u32[]{:S(2)}, u32[]{:S(2)}) collective-permute-start(f32[64,512]{1,0:T(8,128)S(1)} %add.11.chip_ref), channel_id=1, source_target_pairs={{0,8},{8,0},{1,9},{9,1},{2,10},{10,2},{3,11},{11,3},{4,12},{12,4},... | collective-permute-start | bytes 393224 | tf_op jit(solution)/shard_map/ppermute | solution.py:142
  18.0 0.0 copy-done
  18.0 0.0 copy-done.2
  18.0 0.5 convolution_multiply_fusion
  18.5 1.9 %collective-permute-start.3 = (f32[64,256]{1,0:T(8,128)S(1)}, f32[64,256]{1,0:T(8,128)S(1)}, u32[]{:S(2)}, u32[]{:S(2)}) collective-permute-start(f32[64,256]{1,0:T(8,128)S(1)} %convolution_multiply_fusion), channel_id=1, source_target_pairs={{0,8},{1,0},{2,12},{3,4},{4,9},{5,1},{6,13},{7,5},{8,10},{9,2},{10... | collective-permute-start | bytes 196616 | tf_op jit(solution)/shard_map/ppermute | solution.py:146
  20.4 3.8 %collective-permute-start.2 = (f32[64,256]{1,0:T(8,128)S(1)}, f32[64,256]{1,0:T(8,128)S(1)}, u32[]{:S(2)}, u32[]{:S(2)}) collective-permute-start(f32[64,256]{1,0:T(8,128)S(1)} %convolution_multiply_fusion), channel_id=1, source_target_pairs={{0,0},{1,8},{2,4},{3,12},{4,1},{5,9},{6,5},{7,13},{8,2},{9,10},{10... | collective-permute-start | bytes 196616 | tf_op jit(solution)/shard_map/ppermute | solution.py:145
  24.3 2.9 %collective-permute-done.3.b_ref = f32[64,256]{1,0:T(8,128)S(1)} collective-permute-done((f32[64,256]{1,0:T(8,128)S(1)}, f32[64,256]{1,0:T(8,128)S(1)}, u32[]{:S(2)}, u32[]{:S(2)}) %collective-permute-start.3) | collective-permute-done | bytes 65568 | tf_op jit(solution)/shard_map/ppermute | solution.py:146
  27.2 1.3 %collective-permute-done.2.a_ref = f32[64,256]{1,0:T(8,128)S(1)} collective-permute-done((f32[64,256]{1,0:T(8,128)S(1)}, f32[64,256]{1,0:T(8,128)S(1)}, u32[]{:S(2)}, u32[]{:S(2)}) %collective-permute-start.2) | collective-permute-done | bytes 65568 | tf_op jit(solution)/shard_map/ppermute | solution.py:145
  28.5 0.0 collective-permute-done.1.other_ref
  28.5 0.3 shard_map.76
  28.8 10.6 %all_to_all.10.every_ref = f32[8,8,128]{2,1,0:T(8,128)S(1)} all-to-all(f32[8,8,128]{2,1,0:T(8,128)S(1)} %get-tuple-element.10), channel_id=1, replica_groups=mesh['dp'=32,'zh'=2,'co'=2,'zl'=4] {'zl','co'}, dimensions={0} | all-to-all | bytes 65536 | tf_op jit(solution)/shard_map/all_to_all | solution.py:154
  39.3 0.0 copy-done.1
  39.3 0.6 merge.1
  39.9 0.1 shard_map.77.refs_2_
  40.0 2.7 %collective-permute-start.4 = (f32[64,512]{1,0:T(8,128)S(1)}, f32[64,512]{1,0:T(8,128)S(1)}, u32[]{:S(2)}, u32[]{:S(2)}) collective-permute-start(f32[64,512]{1,0:T(8,128)S(1)} %shard_map.77.refs_2_), channel_id=1, source_target_pairs={{0,4},{4,0},{1,5},{5,1},{2,6},{6,2},{3,7},{7,3},{8,12},{12,8},{9,1... | collective-permute-start | bytes 393224 | tf_op jit(solution)/shard_map/ppermute | solution.py:173
  42.7 13.5 %all_to_all.11.refs_4_ = f32[32,1,128]{2,1,0:T(1,128)S(1)} all-to-all(f32[32,1,128]{2,1,0:T(1,128)S(1)} %get-tuple-element.14), channel_id=1, replica_groups={{352,496,320,480,64,448,240,336,464,112,192,368,0,416,176,96,208,160,80..., dimensions={0} | all-to-all | bytes 32768 | tf_op jit(solution)/shard_map/all_to_all | solution.py:168
  56.2 0.0 collective-permute-done.4.refs_3_
  56.2 0.9 %shard_map.78 = (f32[64,1024]{1,0:T(8,128)}, f32[1,1]{1,0:T(1,128)}) custom-call(s32[1]{0:T(128)} %bitcast.5.refs_0_, s32[1]{0:T(128)} %bitcast.zh_ref.refs_1_, f32[64,512]{1,0:T(8,128)S(1)} %shard_map.77.refs_2_, f32[64,512]{1,0:T(8,128)S(1)} %collective-permute-done.4.refs_3_, f32[32,1,128]{2,1,0:T(1,128)S(1)} %all_to_all.11.refs_4_, ...), custom_call_target="tpu_custom_call" | custom-call | tf_op jit(solution)/shard_map/pallas_call | solution.py:178
  (1 shorter events, 0.0 us)
Async XLA Ops:
  0.6 17.3 %copy-start = (bf16[4608,256]{1,0:T(8,128)(2,1)S(1)}, bf16[4608,256]{1,0:T(8,128)(2,1)}, u32[]{:S(2)}) copy-start(bf16[4608,256]{1,0:T(8,128)(2,1)} %param.6) | copy-start | bytes 7077892
  0.6 17.3 %copy-start.2 = (bf16[64,4608]{1,0:T(8,128)(2,1)S(1)}, bf16[64,4608]{1,0:T(8,128)(2,1)}, u32[]{:S(2)}) copy-start(bf16[64,4608]{1,0:T(8,128)(2,1)} %param.5) | copy-start | bytes 1769476
  2.3 10.3 %collective-permute-start = (f32[64,512]{1,0:T(8,128)S(1)}, f32[64,512]{1,0:T(8,128)S(1)}, u32[]{:S(2)}, u32[]{:S(2)}) collective-permute-start(f32[64,512]{1,0:T(8,128)S(1)} %convolution_bitcast_fusion), channel_id=1, source_target_pairs={{0,4},{4,0},{1,5},{5,1},{2,6},{6,2},{3,7},{7,3},{8,12},{12,8},{9,1... | collective-permute-start | bytes 393224 | tf_op jit(solution)/shard_map/ppermute | solution.py:139
  12.7 26.7 %copy-start.1 = (s32[64]{0:T(128)S(1)}, s32[64]{0:T(128)}, u32[]{:S(2)}) copy-start(s32[64]{0:T(128)} %param.9) | copy-start | bytes 772
  12.7 15.8 %collective-permute-start.1 = (f32[64,512]{1,0:T(8,128)S(1)}, f32[64,512]{1,0:T(8,128)S(1)}, u32[]{:S(2)}, u32[]{:S(2)}) collective-permute-start(f32[64,512]{1,0:T(8,128)S(1)} %add.11.chip_ref), channel_id=1, source_target_pairs={{0,8},{8,0},{1,9},{9,1},{2,10},{10,2},{3,11},{11,3},{4,12},{12,4},... | collective-permute-start | bytes 393224 | tf_op jit(solution)/shard_map/ppermute | solution.py:142
  18.5 8.7 %collective-permute-start.3 = (f32[64,256]{1,0:T(8,128)S(1)}, f32[64,256]{1,0:T(8,128)S(1)}, u32[]{:S(2)}, u32[]{:S(2)}) collective-permute-start(f32[64,256]{1,0:T(8,128)S(1)} %convolution_multiply_fusion), channel_id=1, source_target_pairs={{0,8},{1,0},{2,12},{3,4},{4,9},{5,1},{6,13},{7,5},{8,10},{9,2},{10... | collective-permute-start | bytes 196616 | tf_op jit(solution)/shard_map/ppermute | solution.py:146
  20.4 8.1 %collective-permute-start.2 = (f32[64,256]{1,0:T(8,128)S(1)}, f32[64,256]{1,0:T(8,128)S(1)}, u32[]{:S(2)}, u32[]{:S(2)}) collective-permute-start(f32[64,256]{1,0:T(8,128)S(1)} %convolution_multiply_fusion), channel_id=1, source_target_pairs={{0,0},{1,8},{2,4},{3,12},{4,1},{5,9},{6,5},{7,13},{8,2},{9,10},{10... | collective-permute-start | bytes 196616 | tf_op jit(solution)/shard_map/ppermute | solution.py:145
  40.0 16.2 %collective-permute-start.4 = (f32[64,512]{1,0:T(8,128)S(1)}, f32[64,512]{1,0:T(8,128)S(1)}, u32[]{:S(2)}, u32[]{:S(2)}) collective-permute-start(f32[64,512]{1,0:T(8,128)S(1)} %shard_map.77.refs_2_), channel_id=1, source_target_pairs={{0,4},{4,0},{1,5},{5,1},{2,6},{6,2},{3,7},{7,3},{8,12},{12,8},{9,1... | collective-permute-start | bytes 393224 | tf_op jit(solution)/shard_map/ppermute | solution.py:173
